TPU v7x, 32 devices: a whole 2x2x4 slice. The times are simulated.
32 devices in a mesh: tube: 4 (over z), col: 2 (over y), row: 4 (over x, core).
Axes of the slice: x: 2, y: 2, z: 4, core: 2. Of those that a mesh axis runs over, the one named last changes fastest.
Arguments:
- tensor: float32 [16, 2048, 8192], P('tube', 'row', 'col')
- b_init: float32 [8192, 256], P(('col', 'row', 'tube'))
- c_init: float32 [16, 256], replicated
- ridge_lam: float32 [], replicated
Outputs:
- output 1: float32 [2048, 256], P(('row', 'col', 'tube'))
- output 2: float32 [8192, 256], P(('col', 'row', 'tube'))
- output 3: float32 [16, 256], replicated
All inputs are finite; a program needn't handle non-finite values.
Results may differ from a plain program's by a relative error of at most 0.00544.
Values are sent between devices in bfloat16 or wider.
A program may use at most 1 GiB of HBM per device.

v0:
```python
import jax
import jax.numpy as jnp
from jax import lax
from jax.sharding import PartitionSpec as P, NamedSharding

SWEEPS = 2
ALL_AXES = ("tube", "col", "row")


def gram_of(factor):
    half_fac = factor.astype(jnp.bfloat16)
    return lax.dot_general(half_fac, half_fac, (((0,), (0,)), ((), ())), preferred_element_type=jnp.float32)


def solve_rows(mttkrp_rows, gram_prod, ridge_lam):
    ident_mat = jnp.eye(gram_prod.shape[0], dtype=jnp.float32)
    chol_fac = jnp.linalg.cholesky(gram_prod + ridge_lam * ident_mat)
    half_solve = lax.linalg.triangular_solve(chol_fac, mttkrp_rows, left_side=False, lower=True, transpose_a=True)
    return lax.linalg.triangular_solve(chol_fac, half_solve, left_side=False, lower=True)


def solution(mesh):
    full_prec = lax.Precision.HIGHEST

    def local_sweeps(x_blk, b_own, c_full, ridge_lam):
        k_loc, i_loc, j_loc = x_blk.shape
        cp_rank = b_own.shape[1]
        x_half = x_blk.astype(jnp.bfloat16)
        flat_x = x_half.reshape(k_loc * i_loc, j_loc)
        tube_idx = lax.axis_index("tube")
        b_cols = lax.all_gather(b_own, ("row", "tube"), axis=0, tiled=True)
        gram_b = lax.psum(gram_of(b_own), ALL_AXES)
        for sweep_idx in range(SWEEPS):
            c_blk = lax.dynamic_slice_in_dim(c_full, tube_idx * k_loc, k_loc, 0)
            gram_c = gram_of(c_full)
            u_kir = jnp.dot(flat_x, b_cols.astype(jnp.bfloat16), preferred_element_type=jnp.float32).reshape(k_loc, i_loc, cp_rank)
            part_a = jnp.einsum("kir,kr->ir", u_kir, c_blk, preferred_element_type=jnp.float32, precision=full_prec)
            mtt_a = lax.psum_scatter(part_a, ("col", "tube"), scatter_dimension=0, tiled=True)
            a_own = solve_rows(mtt_a, gram_b * gram_c, ridge_lam)
            gram_a = lax.psum(gram_of(a_own), ALL_AXES)
            a_rows = lax.all_gather(a_own, ("col", "tube"), axis=0, tiled=True)
            v_kjr = jnp.einsum("kij,ir->kjr", x_half, a_rows.astype(jnp.bfloat16), preferred_element_type=jnp.float32)
            part_b = jnp.einsum("kjr,kr->jr", v_kjr, c_blk, preferred_element_type=jnp.float32, precision=full_prec)
            mtt_b = lax.psum_scatter(part_b, ("row", "tube"), scatter_dimension=0, tiled=True)
            b_own = solve_rows(mtt_b, gram_a * gram_c, ridge_lam)
            gram_b = lax.psum(gram_of(b_own), ALL_AXES)
            b_cols = lax.all_gather(b_own, ("row", "tube"), axis=0, tiled=True)
            u_kir = jnp.dot(flat_x, b_cols.astype(jnp.bfloat16), preferred_element_type=jnp.float32).reshape(k_loc, i_loc, cp_rank)
            part_c = jnp.einsum("kir,ir->kr", u_kir, a_rows, preferred_element_type=jnp.float32, precision=full_prec)
            c_local = lax.psum(part_c, ("row", "col"))
            mtt_c = lax.all_gather(c_local, "tube", axis=0, tiled=True)
            c_full = solve_rows(mtt_c, gram_a * gram_b, ridge_lam)
        return a_own, b_own, c_full

    return jax.shard_map(
        local_sweeps,
        mesh=mesh,
        in_specs=(P("tube", "row", "col"), P(("col", "row", "tube"), None), P(None, None), P()),
        out_specs=(P(("row", "col", "tube"), None), P(("col", "row", "tube"), None), P(None, None)),
        check_vma=False,
    )
```

profile of v0, /device:TPU:0, one launch (start us, length us, event | category | flops | bytes accessed | tf_op | source)
XLA Modules:
  0.0 1304.4 jit_solution(17838979826806511810)
XLA Ops:
  11.8 17.4 %convert_element_type.48 = bf16[4,512,4096]{2,1,0:T(8,128)(2,1)} convert(f32[4,512,4096]{2,1,0:T(8,128)} %param.17) | non-fusion elementwise | flops 8388608 | bytes 50331648 | tf_op jit(solution)/shard_map/convert_element_type | solution.py:28
  29.9 118.0 %all-reduce.7.cloned.1.call-done = f32[256,256]{0,1:T(8,128)} async-done(((f32[256,256]{0,1:T(8,128)}), f32[256,256]{0,1:T(8,128)}) %all-reduce.7.cloned.1.call-update) | async-done | bytes 262160 | tf_op jit(solution)/shard_map/psum | solution.py:32
  149.3 11.7 cholesky.298
  161.1 9.8 custom-call.37
  171.3 11.7 cholesky.315
  183.1 12.2 multiply_reduce_fusion.4
  201.4 19.7 %custom-call.38 = f32[2,128,128]{1,2,0:T(8,128)S(1)} custom-call(f32[2,128,128]{2,1,0:T(8,128)S(1)} %get-tuple-element.94), custom_call_target="InvertDiagBlocksLowerTriangular" | custom-call | tf_op jit(solution)/shard_map/triangular_solve/custom-call.0 | solution.py:18
  221.1 36.3 %reduce-scatter.13.cloned.1.call-done = f32[64,256]{1,0:T(8,128)} async-done(((f32[512,256]{1,0:T(8,128)}), f32[64,256]{1,0:T(8,128)}) %reduce-scatter.13.cloned.1.call-update) | async-done | bytes 65552 | tf_op jit(solution)/shard_map/reduce_scatter | solution.py:38
  261.1 32.5 %all_gather.22 = f32[512,256]{1,0:T(8,128)S(1)} all-gather(f32[64,256]{1,0:T(8,128)S(1)} %pad_maximum_fusion.2), channel_id=1, replica_groups=mesh['tube'=4,'col'=2,'row'=4] {'col','tube'}, dimensions={0}, use_global_device_ids=true | all-gather | bytes 589824 | tf_op jit(solution)/shard_map/all_gather | solution.py:41
  293.7 15.3 %multiply_reduce_fusion.1 = f32[256,4096]{1,0:T(8,128)} fusion(bf16[4,512,4096]{2,1,0:T(8,128)(2,1)} %convert_element_type.48, f32[256,4]{0,1:T(4,128)S(1)} %dynamic-slice_bitcast_fusion, f32[512,256]{1,0:T(8,128)S(1)} %all_gather.22), kind=kOutput, calls=%fused_computation.13 | convolution fusion | flops 4302438400 | bytes 21499904 | tf_op jit(solution)/shard_map/kij,ir->kjr/dot_general | solution.py:42
  309.0 5.6 copy.78
  314.9 110.8 %all-reduce.9.cloned.1.call-done = f32[256,256]{0,1:T(8,128)} async-done(((f32[256,256]{0,1:T(8,128)}), f32[256,256]{0,1:T(8,128)}) %all-reduce.9.cloned.1.call-update) | async-done | bytes 262160 | tf_op jit(solution)/shard_map/psum | solution.py:40
  426.9 11.7 cholesky.332
  438.7 9.8 custom-call.40
  449.0 11.7 cholesky.349
  463.5 4.1 while.25
  467.6 19.7 %custom-call.41 = f32[2,128,128]{1,2,0:T(8,128)S(1)} custom-call(f32[2,128,128]{2,1,0:T(8,128)S(1)} %get-tuple-element.96), custom_call_target="InvertDiagBlocksLowerTriangular" | custom-call | tf_op jit(solution)/shard_map/triangular_solve/custom-call.5 | solution.py:18
  493.4 127.7 %all-reduce.11.cloned.1.call-done = f32[256,256]{0,1:T(8,128)} async-done(((f32[256,256]{0,1:T(8,128)}), f32[256,256]{0,1:T(8,128)}) %all-reduce.11.cloned.1.call-update) | async-done | bytes 262160 | tf_op jit(solution)/shard_map/psum | solution.py:46
  622.3 11.7 cholesky.366
  634.1 9.8 custom-call.43
  644.4 11.7 cholesky.383
  658.8 4.1 while.26
  662.9 19.7 %custom-call.44 = f32[2,128,128]{1,2,0:T(8,128)S(1)} custom-call(f32[2,128,128]{2,1,0:T(8,128)S(1)} %get-tuple-element.98), custom_call_target="InvertDiagBlocksLowerTriangular" | custom-call | tf_op jit(solution)/shard_map/triangular_solve/custom-call.7 | solution.py:18
  682.7 12.2 convolution_bitcast_fusion.1
  698.3 13.4 %psum.52 = f32[4,256]{1,0:T(4,128)S(1)} all-reduce(f32[4,256]{1,0:T(4,128)S(1)} %bitcast.346), channel_id=1, replica_groups=mesh['tube'=4,'col'=2,'row'=4] {'row','col'}, use_global_device_ids=true, to_apply=%region_9.15 | all-reduce | flops 1024 | bytes 8192 | tf_op jit(solution)/shard_map/psum | solution.py:50
  711.6 13.3 %all-gather = f32[4,4,256]{2,1,0:T(4,128)S(1)} all-gather(f32[1,4,256]{2,1,0:T(4,128)S(1)} %bitcast.347), channel_id=1, replica_groups=mesh['tube'=4,'col'=2,'row'=4] {'tube'}, dimensions={0}, use_global_device_ids=true | all-gather | bytes 20480 | tf_op jit(solution)/shard_map/all_gather | solution.py:51
  726.5 11.7 cholesky.400
  738.3 9.8 custom-call.46
  748.6 11.7 cholesky.417
  772.6 19.7 %custom-call.47 = f32[2,128,128]{1,2,0:T(8,128)S(1)} custom-call(f32[2,128,128]{2,1,0:T(8,128)S(1)} %get-tuple-element.100), custom_call_target="InvertDiagBlocksLowerTriangular" | custom-call | tf_op jit(solution)/shard_map/triangular_solve/custom-call.0 | solution.py:18
  792.3 35.7 %reduce-scatter.15.cloned.1.call-done = f32[64,256]{1,0:T(8,128)} async-done(((f32[512,256]{1,0:T(8,128)}), f32[64,256]{1,0:T(8,128)}) %reduce-scatter.15.cloned.1.call-update) | async-done | bytes 65552 | tf_op jit(solution)/shard_map/reduce_scatter | solution.py:38
  830.9 32.5 %all_gather.25 = f32[512,256]{1,0:T(8,128)S(1)} all-gather(f32[64,256]{1,0:T(8,128)S(1)} %pad_maximum_fusion.3), channel_id=1, replica_groups=mesh['tube'=4,'col'=2,'row'=4] {'col','tube'}, dimensions={0}, use_global_device_ids=true | all-gather | bytes 589824 | tf_op jit(solution)/shard_map/all_gather | solution.py:41
  864.3 15.3 %multiply_reduce_fusion = f32[256,4096]{1,0:T(8,128)} fusion(bf16[4,512,4096]{2,1,0:T(8,128)(2,1)} %convert_element_type.48, f32[256,4]{0,1:T(4,128)S(1)} %get-tuple-element.201, f32[512,256]{1,0:T(8,128)S(1)} %all_gather.25), kind=kOutput, calls=%fused_computation.12 | convolution fusion | flops 4302438400 | bytes 21499904 | tf_op jit(solution)/shard_map/kij,ir->kjr/dot_general | solution.py:42
  879.6 5.6 copy.97
  885.5 110.9 %all-reduce.13.cloned.1.call-done = f32[256,256]{0,1:T(8,128)} async-done(((f32[256,256]{0,1:T(8,128)}), f32[256,256]{0,1:T(8,128)}) %all-reduce.13.cloned.1.call-update) | async-done | bytes 262160 | tf_op jit(solution)/shard_map/psum | solution.py:40
  997.6 11.7 cholesky.434
  1009.4 9.8 custom-call.49
  1019.6 11.7 cholesky.451
  1037.8 19.7 %custom-call.50 = f32[2,128,128]{1,2,0:T(8,128)S(1)} custom-call(f32[2,128,128]{2,1,0:T(8,128)S(1)} %get-tuple-element.102), custom_call_target="InvertDiagBlocksLowerTriangular" | custom-call | tf_op jit(solution)/shard_map/triangular_solve/custom-call.5 | solution.py:18
  1064.2 127.3 %all-reduce.15.cloned.1.call-done = f32[256,256]{0,1:T(8,128)} async-done(((f32[256,256]{0,1:T(8,128)}), f32[256,256]{0,1:T(8,128)}) %all-reduce.15.cloned.1.call-update) | async-done | bytes 262160 | tf_op jit(solution)/shard_map/psum | solution.py:46
  1192.7 11.7 cholesky.468
  1204.5 9.8 custom-call.52
  1214.8 11.7 cholesky.485
  1229.1 4.2 while.29
  1233.3 19.7 %custom-call.53 = f32[2,128,128]{1,2,0:T(8,128)S(1)} custom-call(f32[2,128,128]{2,1,0:T(8,128)S(1)} %get-tuple-element.104), custom_call_target="InvertDiagBlocksLowerTriangular" | custom-call | tf_op jit(solution)/shard_map/triangular_solve/custom-call.7 | solution.py:18
  1253.0 12.2 convolution_bitcast_fusion
  1268.6 13.4 %psum.55 = f32[4,256]{1,0:T(4,128)S(1)} all-reduce(f32[4,256]{1,0:T(4,128)S(1)} %bitcast.348), channel_id=1, replica_groups=mesh['tube'=4,'col'=2,'row'=4] {'row','col'}, use_global_device_ids=true, to_apply=%region_14.22 | all-reduce | flops 1024 | bytes 8192 | tf_op jit(solution)/shard_map/psum | solution.py:50
  1282.0 13.0 all-gather.1
  (220 shorter events, 92.6 us)
Async XLA Ops:
  8.0 139.9 %all-reduce.7.cloned.1.call-start = ((), (), s32[]{:S(2)}) async-start(), calls=%async_computation.4 | async-start | bytes 524288 | tf_op jit(solution)/shard_map/psum | solution.py:32
  10.0 173.1 %all-gather.6.cloned.1.call-start = ((), (), s32[]{:S(2)}) async-start(), calls=%async_computation.5 | async-start | bytes 2228224 | tf_op jit(solution)/shard_map/all_gather | solution.py:31
  11.7 245.6 %reduce-scatter.13.cloned.1.call-start = ((), (), s32[]{:S(2)}) async-start(), calls=%async_computation.14 | async-start | bytes 589824 | tf_op jit(solution)/shard_map/reduce_scatter | solution.py:38
  11.8 18.1 %copy-start.4 = (f32[16,256]{1,0:T(8,128)S(1)}, f32[16,256]{1,0:T(8,128)}, u32[]{:S(2)}) copy-start(f32[16,256]{1,0:T(8,128)} %param.19) | copy-start | bytes 49156
  195.3 230.4 %all-reduce.9.cloned.1.call-start = ((), (), s32[]{:S(2)}) async-start(), calls=%async_computation.6 | async-start | bytes 524288 | tf_op jit(solution)/shard_map/psum | solution.py:40
  293.7 193.6 %reduce-scatter.9.cloned.1.call-start = ((), (), s32[]{:S(2)}) async-start(), calls=%async_computation.7 | async-start | bytes 4456448 | tf_op jit(solution)/shard_map/reduce_scatter | solution.py:44
  314.6 306.5 %all-reduce.11.cloned.1.call-start = ((), (), s32[]{:S(2)}) async-start(), calls=%async_computation.8 | async-start | bytes 524288 | tf_op jit(solution)/shard_map/psum | solution.py:46
  488.5 132.6 %copy-start.1 = (f32[256,256]{0,1:T(8,128)S(1)}, f32[256,256]{0,1:T(8,128)}, u32[]{:S(2)}) copy-start(f32[256,256]{0,1:T(8,128)} %all-reduce.9.cloned.1.call-done) | copy-start | bytes 786436
  492.0 190.7 %all-gather.8.cloned.1.call-start = ((), (), s32[]{:S(2)}) async-start(), calls=%async_computation.9 | async-start | bytes 2228224 | tf_op jit(solution)/shard_map/all_gather | solution.py:47
  492.7 335.3 %reduce-scatter.15.cloned.1.call-start = ((), (), s32[]{:S(2)}) async-start(), calls=%async_computation.15 | async-start | bytes 589824 | tf_op jit(solution)/shard_map/reduce_scatter | solution.py:38
  697.6 28.5 %copy-start.2 = (f32[256,256]{0,1:T(8,128)S(1)}, f32[256,256]{0,1:T(8,128)}, u32[]{:S(2)}) copy-start(f32[256,256]{0,1:T(8,128)} %all-reduce.11.cloned.1.call-done) | copy-start | bytes 786436
  765.8 230.6 %all-reduce.13.cloned.1.call-start = ((), (), s32[]{:S(2)}) async-start(), calls=%async_computation.10 | async-start | bytes 524288 | tf_op jit(solution)/shard_map/psum | solution.py:40
  830.9 48.8 %copy-start.3 = (f32[64,256]{1,0:T(8,128)}, f32[64,256]{1,0:T(8,128)S(1)}, u32[]{:S(2)}) copy-start(f32[64,256]{1,0:T(8,128)S(1)} %pad_maximum_fusion.3) | copy-start | bytes 196612
  864.3 193.2 %reduce-scatter.11.cloned.1.call-start = ((), (), s32[]{:S(2)}) async-start(), calls=%async_computation.11 | async-start | bytes 4456448 | tf_op jit(solution)/shard_map/reduce_scatter | solution.py:44
  885.3 306.3 %all-reduce.15.cloned.1.call-start = ((), (), s32[]{:S(2)}) async-start(), calls=%async_computation.12 | async-start | bytes 524288 | tf_op jit(solution)/shard_map/psum | solution.py:46
  1060.4 131.1 %copy-start = (f32[256,256]{0,1:T(8,128)S(1)}, f32[256,256]{0,1:T(8,128)}, u32[]{:S(2)}) copy-start(f32[256,256]{0,1:T(8,128)} %all-reduce.13.cloned.1.call-done) | copy-start | bytes 786436
  1062.2 190.8 %all-gather.10.cloned.1.call-start = ((), (), s32[]{:S(2)}) async-start(), calls=%async_computation.13 | async-start | bytes 2228224 | tf_op jit(solution)/shard_map/all_gather | solution.py:47
Sparse Core Ops, SparseCore 0:
  14.9 132.9 all-reduce.6
  293.8 131.8 all-reduce.8
  492.1 128.9 all-reduce.10
  864.4 131.9 all-reduce.12
  1062.3 129.1 all-reduce.14
Sparse Core Ops, SparseCore 1:
  12.7 44.4 all-gather.5
  195.4 61.9 reduce-scatter.12
  314.7 72.0 reduce-scatter.8
  494.9 40.3 all-gather.7
  765.9 62.1 reduce-scatter.14
  885.3 72.1 reduce-scatter.10
  1064.8 40.3 all-gather.9
where the time goes:
time: 1310 us; the launch traced here: 1300 us
  waiting for transfers between devices  667 us (51%)
  other arithmetic  352 us (27%)
  blocking collectives  118 us (9%)
  matrix products  96.4 us (7%)
  local copies, waits for them, and re-layouts  43.9 us (3%)
  between operations  25 us (2%)
    psum x3, waiting for transfers between devices, local_sweeps(): gram_b = lax.psum(gram_of(b_own), ALL_AXES)  373 us
    psum x2, waiting for transfers between devices, local_sweeps(): gram_a = lax.psum(gram_of(a_own), ALL_AXES)  222 us
    another operation x41, other arithmetic, solve_rows(): chol_fac = jnp.linalg.cholesky(gram_prod + ridge_lam * ident_mat)  207 us
    another operation x13, other arithmetic, solve_rows(): lax.linalg.triangular_solve(chol_fac, mttkrp_rows, left_side=False, lower...  118 us
    reduce_scatter x2, waiting for transfers between devices, local_sweeps(): lax.psum_scatter(part_a, ('col', 'tube'), scatter_dimension=0, tiled=True)  72 us
    all_gather x2, blocking collectives, local_sweeps(): a_rows = lax.all_gather(a_own, ('col', 'tube'), axis=0, tiled=True)  65 us
    dot_general x3, matrix products, local_sweeps(): jnp.dot(flat_x, b_cols.astype(jnp.bfloat16), preferred_element_type=jnp.f...  36.6 us
    dot_general x2, matrix products, local_sweeps(): jnp.einsum('kij,ir->kjr', x_half, a_rows.astype(jnp.bfloat16), preferred_...  30.6 us
  transfers between devices with their start and end apart: 12, of which 7 were waited for; matrix products, arithmetic and copies ran while one was open for 30% of the time, Pallas kernels for 0%

commit v1 on v0

v1 whole, which is shorter than its diff:
```python
import jax
import jax.numpy as jnp
from jax import lax
from jax.experimental import pallas as pl
from jax.experimental.pallas import tpu as pltpu
from jax.sharding import PartitionSpec as P

SWEEPS = 2
F32 = jnp.float32
BF16 = jnp.bfloat16
HI = lax.Precision.HIGHEST
MESH = pl.DeviceIdType.MESH
RANK = 256
PIV = 16
ROWS_T = 64
STAGES = 4


def dot32(lhs, rhs, lhs_dim, rhs_dim):
    return lax.dot_general(lhs, rhs, (((lhs_dim,), (rhs_dim,)), ((), ())), precision=HI, preferred_element_type=F32)


def dot16(lhs, rhs, lhs_dim, rhs_dim):
    return lax.dot_general(lhs, rhs, (((lhs_dim,), (rhs_dim,)), ((), ())), preferred_element_type=F32)


def factor_block(blk, w_ref, inv_ref, idx):
    size = 128
    lane = lax.broadcasted_iota(jnp.int32, (PIV, size), 1)
    row = lax.broadcasted_iota(jnp.int32, (PIV, size), 0)
    lanes = lax.broadcasted_iota(jnp.int32, (size, size), 1)
    lo = pl.multiple_of(blk * PIV, PIV)
    slab = w_ref[pl.ds(lo, PIV)]
    full = w_ref[...]
    cols = jnp.stack([jnp.broadcast_to(slab[:, q:q + 1], (PIV, size)) for q in range(PIV)])
    work = pltpu.roll(jnp.where(lane < PIV, jnp.where(lane == row, 1.0, 0.0), slab), size - PIV, 1)
    rest = pltpu.roll(jnp.where(lanes < PIV, 0.0, full), size - PIV, 1)
    scale = jnp.ones((PIV, size), F32)
    low = work
    for q in range(PIV):
        here = row == q
        piv = cols[0, q:q + 1]
        rec = 1.0 / piv
        mult = jnp.where(here, 0.0, cols[0] * rec)
        low = jnp.where(here, work * lax.rsqrt(piv), low)
        scale = jnp.where(here, rec, scale)
        work = work - mult * work[q:q + 1]
        if q + 1 < PIV:
            cols = cols[1:] - mult[None] * cols[1:, q:q + 1]
    mid = work * scale
    for q in range(PIV):
        rest = rest - full[:, q:q + 1] * mid[q:q + 1]
    w_ref[...] = rest
    low = jnp.where(lane >= size - PIV - lo, low, 0.0)
    inv_ref[idx, pl.ds(lo, PIV)] = pltpu.roll(low, lo + PIV, 1)


def inv_chol(mat, w_ref, inv_ref, low_ref):
    below = mat[128:, :128]
    corner = mat[128:, 128:]
    w_ref[...] = mat[:128, :128]

    def step(idx, carry):
        lax.fori_loop(0, 128 // PIV, lambda blk, c: (factor_block(blk, w_ref, inv_ref, idx), c)[1], 0)
        low = dot32(below, inv_ref[idx], 1, 1)
        low_ref[idx] = low
        w_ref[...] = corner - dot32(low, low, 1, 1)
        return carry

    lax.fori_loop(0, 2, step, 0)
    first, second = inv_ref[0], inv_ref[1]
    off = -dot32(dot32(second, low_ref[0], 1, 0), first, 1, 0)
    top = jnp.concatenate([first, jnp.zeros((128, 128), F32)], axis=1)
    return jnp.concatenate([top, jnp.concatenate([off, second], axis=1)], axis=0)


def kernel(x_ref, b_ref, c_ref, lam_ref, a_out, b_out, c_out,
           xh, xin, u_buf, pa, pb, ball, a16, a32, ya, za, yb, xb, zb,
           gown, gcore, gpeer, gfin, cmid, cpart, ctot, csplat, at_buf, work, hinv, hlow, linv, gmat_a, gmat_b, c_cur,
           load_sem, s_ab, r_ab, s_a16, r_a16, s_a32, r_a32, s_ya, r_ya, s_za, r_za,
           s_yb, r_yb, s_xb, r_xb, s_zb, r_zb, s_g, r_g, s_c, r_c):
    tube = lax.axis_index("tube")
    col = lax.axis_index("col")
    row = lax.axis_index("row")
    core = lax.rem(row, 2)
    xpos = row // 2
    xrow = lax.rem(row + 2, 4)
    crow = row + 1 - 2 * core
    lam = lam_ref[...]

    def dev(t, c, r):
        return {"tube": t, "col": c, "row": r}

    def shift(d):
        return lax.rem(tube + d, 4)

    peer_x, peer_core, peer_y = dev(tube, col, xrow), dev(tube, col, crow), dev(tube, 1 - col, row)

    def peer_z(d):
        return dev(shift(d), col, row)

    def plane(n):
        other = lax.rem(col * 4 + row + n, 8)
        return dev(tube, other // 4, lax.rem(other, 4))

    barrier = pltpu.get_barrier_semaphore()
    for d in range(1, 4):
        pl.semaphore_signal(barrier, inc=1, device_id=peer_z(d), device_id_type=MESH)
    for n in range(1, 8):
        pl.semaphore_signal(barrier, inc=1, device_id=plane(n), device_id_type=MESH)
    pl.semaphore_wait(barrier, 10)

    def remote(src, dst, send, recv, device):
        return pltpu.make_async_remote_copy(src_ref=src, dst_ref=dst, send_sem=send, recv_sem=recv,
                                            device_id=device, device_id_type=MESH)

    def slot_b(r, t):
        return r * 4 + t

    def ab_copy(v, slot, send, device):
        return remote(ball.at[v, slot], ball.at[v, slot], s_ab.at[v, send], r_ab.at[v, slot], device)

    def ab_start(v):
        own = slot_b(row, tube)
        for d in (2, 3, 1):
            ab_copy(v, own, d - 1, peer_z(d)).start()
        ab_copy(v, own, 3, peer_x).start()
        ab_copy(v, own, 4, peer_core).start()

    def ab_relay_z(v, d):
        slot = slot_b(row, shift(d))
        ab_copy(v, slot, 0, peer_x).wait_recv()
        ab_copy(v, slot, 4 + d, peer_x).start()
        ab_copy(v, slot, 7 + d, peer_core).start()

    def ab_relay_x(v, d):
        slot = slot_b(xrow, shift(d))
        ab_copy(v, slot, 0, peer_x).wait_recv()
        ab_copy(v, slot, 11 + d, peer_core).start()

    def ab_core(v):
        for r in (crow, lax.rem(crow + 2, 4)):
            for d in range(4):
                ab_copy(v, slot_b(r, shift(d)), 0, peer_x).wait_recv()

    def ab_finish(v):
        for n in range(15):
            ab_copy(v, 0, n, peer_x).wait_send()

    def aa_copy(buf, s_sem, r_sem, s, slot, send, device):
        return remote(buf.at[s, slot], buf.at[s, slot], s_sem.at[s, send], r_sem.at[s, slot], device)

    def aa_start(buf, s_sem, r_sem, s):
        own = col * 4 + tube
        for d in (2, 3, 1):
            aa_copy(buf, s_sem, r_sem, s, own, d - 1, peer_z(d)).start()
        aa_copy(buf, s_sem, r_sem, s, own, 3, peer_y).start()

    def aa_relay(buf, s_sem, r_sem, s):
        for d in (1, 3, 2):
            slot = col * 4 + shift(d)
            aa_copy(buf, s_sem, r_sem, s, slot, 0, peer_y).wait_recv()
            aa_copy(buf, s_sem, r_sem, s, slot, 3 + d, peer_y).start()

    def aa_rest(buf, s_sem, r_sem, s):
        for d in range(4):
            aa_copy(buf, s_sem, r_sem, s, (1 - col) * 4 + shift(d), 0, peer_y).wait_recv()
        for n in range(7):
            aa_copy(buf, s_sem, r_sem, s, 0, n, peer_y).wait_send()

    def solve_matrix(left, right):
        rows = lax.broadcasted_iota(jnp.int32, (RANK, RANK), 0)
        lanes = lax.broadcasted_iota(jnp.int32, (RANK, RANK), 1)
        return left * right + jnp.where(rows == lanes, lam, 0.0)

    def factor(left, right):
        linv[...] = inv_chol(solve_matrix(left, right), work, hinv, hlow)

    def half(q):
        return pl.ds(pl.multiple_of(q * 128, 128), 128)

    def g_swap(g, dest):
        gfin[g, half(core)] = gown[half(core)] + gpeer[g]
        cp = remote(gfin.at[g, half(core)], gfin.at[g, half(core)], s_g.at[g, 2], r_g.at[g, 2], peer_core)
        cp.start()
        remote(gfin.at[g, half(1 - core)], gfin.at[g, half(1 - core)], s_g.at[g, 2], r_g.at[g, 2], peer_core).wait_recv()
        cp.wait_send()
        dest[...] = gfin[g]

    def g_link(g, device):
        return remote(gown.at[half(core)], gpeer.at[g], s_g.at[g, 1], r_g.at[g, 1], device)

    def gram_b_start(v, g):
        gown[half(core)] = jnp.zeros((128, RANK), F32)

        def step(n, carry):
            gown[half(core)] += dot16(ball[v, n, :, half(core)], ball[v, n], 0, 0)
            return carry

        lax.fori_loop(0, 16, step, 0)
        g_link(g, peer_y).start()

    def g_link_wait(g, device):
        g_link(g, device).wait()

    def form_u(v):
        def step(n, carry):
            rows = pl.ds(pl.multiple_of(n * 256, 256), 256)
            u_buf[rows] = dot16(xh[rows], ball[v].reshape(4096, RANK), 1, 0)
            return carry

        lax.fori_loop(0, 8, step, 0)

    def tile(n):
        slot = lax.rem(n, STAGES)
        return pltpu.make_async_copy(x_ref.at[pl.ds(pl.multiple_of(n * ROWS_T, ROWS_T), ROWS_T)], xin.at[slot], load_sem.at[slot])

    n_tiles = 2048 // ROWS_T

    def convert(first, last):
        def step(n, carry):
            tile(n).wait()
            xh[pl.ds(pl.multiple_of(n * ROWS_T, ROWS_T), ROWS_T)] = xin[lax.rem(n, STAGES)].astype(BF16)
            if last < n_tiles:
                tile(n + STAGES).start()
            return carry

        lax.fori_loop(first, last, step, 0)

    ball[0, slot_b(row, tube)] = b_ref[...].astype(BF16)
    for n in range(STAGES):
        tile(n).start()
    c_cur[...] = c_ref[...]
    ab_start(0)
    part = (n_tiles - STAGES) // 4
    convert(0, part)
    ab_relay_z(0, 1)
    convert(part, 2 * part)
    ab_relay_x(0, 0)
    ab_relay_z(0, 3)
    convert(2 * part, 3 * part)
    ab_relay_z(0, 2)
    ab_relay_x(0, 1)
    convert(3 * part, 4 * part)
    convert(4 * part, n_tiles)
    ab_relay_x(0, 3)
    ab_relay_x(0, 2)
    ab_core(0)
    gram_b_start(0, 0)
    form_u(0)
    g_link_wait(0, peer_y)
    g_swap(0, gmat_b)
    ab_finish(0)

    def sweep(s, carry):
        c16 = c_cur[...].astype(BF16)
        gram_c = dot16(c16, c16, 0, 0)
        c_blk = c_cur[0:4]
        for t in range(1, 4):
            c_blk = jnp.where(tube == t, c_cur[4 * t:4 * t + 4], c_blk)

        def ya_copy(t):
            return remote(pa.at[(1 - col) * 4 + t], ya.at[s, t], s_ya.at[s, t], r_ya.at[s, t], peer_y)

        def za_copy(d):
            return remote(pa.at[col * 4 + shift(d)], za.at[s, d - 1], s_za.at[s, d - 1], r_za.at[s, d - 1], peer_z(d))

        def form_pa(slot):
            acc = None
            for k in range(4):
                term = u_buf[pl.ds(pl.multiple_of(k * 512 + slot * 64, 64), 64)] * c_blk[k:k + 1]
                acc = term if acc is None else acc + term
            pa[slot] = acc

        for d in (2, 3, 1, 0):
            form_pa((1 - col) * 4 + shift(d))
            ya_copy(shift(d)).start()
        for d in (2, 3, 1, 0):
            form_pa(col * 4 + shift(d))
        factor(gmat_b[...], gram_c)
        for d in (2, 3, 1):
            ya_copy(shift(d)).wait_recv()
            slot = col * 4 + shift(d)
            pa[slot] = pa[slot] + ya[s, shift(d)]
            za_copy(d).start()
        ya_copy(tube).wait_recv()
        total = pa[col * 4 + tube] + ya[s, tube]
        for d in (1, 3, 2):
            za_copy(d).wait_recv()
            total = total + za[s, d - 1]
        a_own = dot32(dot32(total, linv[...], 1, 1), linv[...], 1, 0)
        own_a = col * 4 + tube
        a32[s, own_a] = a_own
        a16[s, own_a] = a_own.astype(BF16)
        aa_start(a16, s_a16, r_a16, s)
        aa_start(a32, s_a32, r_a32, s)
        for k in range(4):
            csplat[k] = jnp.broadcast_to(c_blk[k:k + 1], (128, RANK)).T
        for t in range(4):
            ya_copy(t).wait_send()
        for d in range(1, 4):
            za_copy(d).wait_send()
        aa_relay(a16, s_a16, r_a16, s)
        aa_rest(a16, s_a16, r_a16, s)
        a_rows = a16[s].reshape(512, RANK)
        at_buf[...] = a_rows.astype(F32).T.astype(BF16)
        gown[...] = dot16(a_rows, a_rows, 0, 0)
        g = 1 + 2 * s
        core_gram = remote(gown.at[half(1 - core)], gcore.at[s], s_g.at[g, 0], r_g.at[g, 0], peer_core)
        core_gram.start()

        def form_pb(slot):
            acc0 = acc1 = None
            for k in range(4):
                xk = xh[k * 512:(k + 1) * 512, pl.ds(pl.multiple_of(slot * 256, 256), 256)]
                val = dot16(at_buf[...], xk, 1, 0)
                left = val[:, :128] * csplat[k]
                right = val[:, 128:] * csplat[k]
                acc0 = left if k == 0 else acc0 + left
                acc1 = right if k == 0 else acc1 + right
            pb[slot] = jnp.concatenate([acc0, acc1], axis=1)

        def order(n):
            return shift((2, 3, 1, 0)[n % 4])

        def chunk(n, q):
            xside = 1 - xpos if n < 4 else xpos
            return slot_b(xside * 2 + q, order(n))

        def yb_copy(n):
            return remote(pb.at[chunk(n, 1 - core)], yb.at[s, n], s_yb.at[s, n], r_yb.at[s, n], peer_core)

        def xb_copy(n):
            return remote(pb.at[chunk(n, core)], xb.at[s, n], s_xb.at[s, n], r_xb.at[s, n], peer_x)

        def zb_copy(d):
            return remote(pb.at[slot_b(row, shift(d))], zb.at[s, d - 1], s_zb.at[s, d - 1], r_zb.at[s, d - 1], peer_z(d))

        def merge_core(n):
            yb_copy(n).wait_recv()
            slot = chunk(n, core)
            pb[slot] = pb[slot] + yb[s, n]
            if n < 4:
                xb_copy(n).start()

        for n in range(8):
            form_pb(chunk(n, 1 - core))
            yb_copy(n).start()
            form_pb(chunk(n, core))
            if n == 0:
                core_gram.wait()
                gown[half(core)] = gown[half(core)] + gcore[s]
                g_link(g, peer_x).start()
            if n >= 1:
                merge_core(n - 1)
        merge_core(7)
        aa_relay(a32, s_a32, r_a32, s)
        g_link_wait(g, peer_x)
        g_swap(g, gmat_a)
        factor(gmat_a[...], gram_c)
        for n in range(3):
            xb_copy(n).wait_recv()
            slot = slot_b(row, order(n))
            pb[slot] = pb[slot] + xb[s, n]
            zb_copy((2, 3, 1)[n]).start()
        aa_rest(a32, s_a32, r_a32, s)
        xb_copy(3).wait_recv()
        total = pb[slot_b(row, tube)] + xb[s, 3]
        for d in (1, 3, 2):
            zb_copy(d).wait_recv()
            total = total + zb[s, d - 1]
        b_own = dot32(dot32(linv[...], total, 1, 0), linv[...], 0, 0)
        b_out[...] = b_own
        v = s + 1
        ball[v, slot_b(row, tube)] = b_own.astype(BF16)
        ab_start(v)
        for n in range(8):
            yb_copy(n).wait_send()
        for n in range(4):
            xb_copy(n).wait_send()
        for d in range(1, 4):
            zb_copy(d).wait_send()
        ab_relay_z(v, 1)
        ab_relay_z(v, 3)
        ab_relay_x(v, 0)
        ab_relay_z(v, 2)
        for d in (1, 3, 2):
            ab_relay_x(v, d)
        ab_core(v)
        gram_b_start(v, g + 1)
        form_u(v)

        cpart[s, 0] = jnp.zeros((8, RANK), F32)
        for k in range(4):
            prod = u_buf[k * 512:(k + 1) * 512] * a32[s].reshape(512, RANK)
            cpart[s, 0, k:k + 1] = jnp.sum(prod, axis=0, keepdims=True)

        def cp_copy(n):
            return remote(cpart.at[s, 0], cpart.at[s, n], s_c.at[s, n], r_c.at[s, n], plane(n))

        def ct_copy(d):
            return remote(ctot.at[s, tube], ctot.at[s, tube], s_c.at[s, 7 + d], r_c.at[s, 7 + d], peer_z(d))

        for n in range(1, 8):
            cp_copy(n).start()
        g_link_wait(g + 1, peer_y)
        g_swap(g + 1, gmat_b)
        for n in range(1, 8):
            cp_copy(n).wait_recv()
        me = col * 4 + row
        total = None
        for n in range(8):
            term = cpart[s, lax.rem(me + 8 - n, 8)]
            total = term if total is None else total + term
        ctot[s, tube] = total
        for d in range(1, 4):
            ct_copy(d).start()
        factor(gmat_a[...], gmat_b[...])
        for d in range(1, 4):
            ct_copy(d).wait_recv()
        cmid[...] = jnp.concatenate([ctot[s, t, :4] for t in range(4)], axis=0)
        c_new = dot32(dot32(cmid[...], linv[...], 1, 1), linv[...], 1, 0)
        c_cur[...] = c_new
        for n in range(1, 8):
            cp_copy(n).wait_send()
        for d in range(1, 4):
            ct_copy(d).wait_send()
        ab_finish(v)
        return carry

    lax.fori_loop(0, SWEEPS, sweep, 0)
    a_out[...] = a32[SWEEPS - 1, col * 4 + tube]
    c_out[...] = c_cur[...]


def solution(mesh):
    dma = pltpu.SemaphoreType.DMA

    def local(x_blk, b_own, c_full, ridge_lam):
        vmem = pl.BlockSpec(memory_space=pltpu.VMEM)
        return pl.pallas_call(
            kernel,
            out_shape=(
                jax.ShapeDtypeStruct((64, RANK), F32),
                jax.ShapeDtypeStruct((256, RANK), F32),
                jax.ShapeDtypeStruct((16, RANK), F32),
            ),
            in_specs=[pl.BlockSpec(memory_space=pl.ANY), vmem, vmem, vmem],
            out_specs=(vmem, vmem, vmem),
            scratch_shapes=[
                pltpu.VMEM((2048, 4096), BF16),
                pltpu.VMEM((STAGES, ROWS_T, 4096), F32),
                pltpu.VMEM((2048, RANK), F32),
                pltpu.VMEM((8, 64, RANK), F32),
                pltpu.VMEM((16, 256, 256), F32),
                pltpu.VMEM((3, 16, 256, RANK), BF16),
                pltpu.VMEM((2, 8, 64, RANK), BF16),
                pltpu.VMEM((2, 8, 64, RANK), F32),
                pltpu.VMEM((2, 4, 64, RANK), F32),
                pltpu.VMEM((2, 3, 64, RANK), F32),
                pltpu.VMEM((2, 8, 256, 256), F32),
                pltpu.VMEM((2, 4, 256, 256), F32),
                pltpu.VMEM((2, 3, 256, 256), F32),
                pltpu.VMEM((RANK, RANK), F32),
                pltpu.VMEM((2, 128, RANK), F32),
                pltpu.VMEM((5, 128, RANK), F32),
                pltpu.VMEM((5, RANK, RANK), F32),
                pltpu.VMEM((16, RANK), F32),
                pltpu.VMEM((2, 8, 8, RANK), F32),
                pltpu.VMEM((2, 4, 8, RANK), F32),
                pltpu.VMEM((4, RANK, 128), F32),
                pltpu.VMEM((RANK, 512), BF16),
                pltpu.VMEM((128, 128), F32),
                pltpu.VMEM((2, 128, 128), F32),
                pltpu.VMEM((2, 128, 128), F32),
                pltpu.VMEM((RANK, RANK), F32),
                pltpu.VMEM((RANK, RANK), F32),
                pltpu.VMEM((RANK, RANK), F32),
                pltpu.VMEM((16, RANK), F32),
                dma((STAGES,)),
                dma((3, 15)), dma((3, 16)),
                dma((2, 7)), dma((2, 8)), dma((2, 7)), dma((2, 8)),
                dma((2, 4)), dma((2, 4)), dma((2, 3)), dma((2, 3)),
                dma((2, 8)), dma((2, 8)), dma((2, 4)), dma((2, 4)), dma((2, 3)), dma((2, 3)),
                dma((5, 3)), dma((5, 3)),
                dma((2, 11)), dma((2, 11)),
            ],
            compiler_params=pltpu.CompilerParams(collective_id=0, has_side_effects=True, vmem_limit_bytes=62 * 1024 * 1024),
        )(x_blk.reshape(2048, 4096), b_own, c_full, jnp.broadcast_to(ridge_lam, (1, RANK)))

    return jax.shard_map(
        local,
        mesh=mesh,
        in_specs=(P("tube", "row", "col"), P(("col", "row", "tube"), None), P(None, None), P()),
        out_specs=(P(("row", "col", "tube"), None), P(("col", "row", "tube"), None), P(None, None)),
        check_vma=False,
    )
```

time: 1310 us -> 280 us (0.21)
  waiting for transfers between devices: 667 us -> 0 us
  other arithmetic: 352 us -> 0 us
  Pallas kernels: 0 us -> 269 us
  blocking collectives: 118 us -> 0 us
  matrix products: 96.4 us -> 0 us
  local copies, waits for them, and re-layouts: 43.9 us -> 5.03 us
  between operations: 25 us -> 1.29 us
    psum x5 -> x0, waiting for transfers between devices: 595 us -> none  [the longest x3 373 us: local_sweeps(): gram_b = lax.psum(gram_of(b_own), ALL_AXES)]
    another operation x58 -> x0, other arithmetic: 327 us -> none  [the longest x41 207 us: solve_rows(): chol_fac = jnp.linalg.cholesky(gram_prod + ridge_lam * ident_mat)]
    pallas_call x0 -> x1, Pallas kernels: none -> 269 us  [local(): pl.pallas_call(kernel, out_shape=(jax.ShapeDtypeStruct((64, RANK), F32),...]
    all_gather x4 -> x0, blocking collectives: 91.3 us -> none  [the longest x2 65 us: local_sweeps(): a_rows = lax.all_gather(a_own, ('col', 'tube'), axis=0, tiled=True)]
    dot_general x13 -> x0, matrix products: 78.4 us -> none  [the longest x3 36.6 us: local_sweeps(): jnp.dot(flat_x, b_cols.astype(jnp.bfloat16), preferred_element_type=jnp.f...]
    reduce_scatter x4 -> x0, waiting for transfers between devices: 72 us -> none  [the longest x2 72 us: local_sweeps(): lax.psum_scatter(part_a, ('col', 'tube'), scatter_dimension=0, tiled=True)]
    psum x2 -> x0, blocking collectives: 26.7 us -> none  [local_sweeps(): c_local = lax.psum(part_c, ('row', 'col'))]
    another operation x55 -> x0, local copies, waits for them, and re-layouts: 23.9 us -> none  [the longest x43 23.7 us: solve_rows(): lax.linalg.triangular_solve(chol_fac, mttkrp_rows, left_side=False, lower...]
  transfers between devices with their start and end apart: 12 -> 0, of which waited for: 7 -> 0; matrix products, arithmetic and copies ran while one was open for 30% -> 0% of each run, Pallas kernels for 0% -> 0%
where the time goes in v1:
time: 280 us; the launch traced here: 275 us
  Pallas kernels  269 us (96%)
  local copies, waits for them, and re-layouts  5.03 us (2%)
    pallas_call x1, Pallas kernels, local(): pl.pallas_call(kernel, out_shape=(jax.ShapeDtypeStruct((64, RANK), F32),...  269 us

profile of v1, /device:TPU:0, one launch (start us, length us, event | category | flops | bytes accessed | tf_op | source)
XLA Modules:
  0.0 275.1 jit_solution(1918416047756112948)
XLA Ops:
  1.3 0.6 broadcast_in_dim.3.lam_ref
  1.8 268.8 %shard_map.67 = (f32[64,256]{1,0:T(8,128)}, f32[256,256]{1,0:T(8,128)}, f32[16,256]{1,0:T(8,128)}) custom-call(f32[2048,4096]{1,0:T(8,128)} %bitcast.1, f32[256,256]{1,0:T(8,128)} %b_ref.1, f32[16,256]{1,0:T(8,128)} %c_ref.1, f32[1,256]{1,0:T(1,128)} %broadcast_in_dim.3.lam_ref), custom_call_target="tpu_custom_call" | custom-call | tf_op jit(solution)/shard_map/pallas_call | solution.py:441
  270.6 1.5 copy.11
  272.1 1.7 copy.12
  273.7 1.3 copy.13

commit v2 on v1

--- a/solution.py
+++ b/solution.py
@@ -13,7 +13,7 @@
 RANK = 256
 PIV = 16
 ROWS_T = 64
-STAGES = 4
+STAGES = 8
 
 
 def dot32(lhs, rhs, lhs_dim, rhs_dim):
@@ -41,7 +41,7 @@
         here = row == q
         piv = cols[0, q:q + 1]
         rec = 1.0 / piv
-        mult = jnp.where(here, 0.0, cols[0] * rec)
+        mult = jnp.where(here, 0.0, cols[0]) * rec
         low = jnp.where(here, work * lax.rsqrt(piv), low)
         scale = jnp.where(here, rec, scale)
         work = work - mult * work[q:q + 1]
@@ -55,28 +55,23 @@
     inv_ref[idx, pl.ds(lo, PIV)] = pltpu.roll(low, lo + PIV, 1)
 
 
-def inv_chol(mat, w_ref, inv_ref, low_ref):
-    below = mat[128:, :128]
-    corner = mat[128:, 128:]
+def inv_chol(mat, w_ref, inv_ref, low_ref, between):
     w_ref[...] = mat[:128, :128]
-
-    def step(idx, carry):
-        lax.fori_loop(0, 128 // PIV, lambda blk, c: (factor_block(blk, w_ref, inv_ref, idx), c)[1], 0)
-        low = dot32(below, inv_ref[idx], 1, 1)
-        low_ref[idx] = low
-        w_ref[...] = corner - dot32(low, low, 1, 1)
-        return carry
-
-    lax.fori_loop(0, 2, step, 0)
+    lax.fori_loop(0, 128 // PIV, lambda blk, c: (factor_block(blk, w_ref, inv_ref, 0), c)[1], 0)
+    low = dot32(mat[128:, :128], inv_ref[0], 1, 1)
+    low_ref[...] = low
+    w_ref[...] = mat[128:, 128:] - dot32(low, low, 1, 1)
+    between()
+    lax.fori_loop(0, 128 // PIV, lambda blk, c: (factor_block(blk, w_ref, inv_ref, 1), c)[1], 0)
     first, second = inv_ref[0], inv_ref[1]
-    off = -dot32(dot32(second, low_ref[0], 1, 0), first, 1, 0)
+    off = -dot32(second, dot32(low_ref[...], first, 1, 0), 1, 0)
     top = jnp.concatenate([first, jnp.zeros((128, 128), F32)], axis=1)
     return jnp.concatenate([top, jnp.concatenate([off, second], axis=1)], axis=0)
 
 
 def kernel(x_ref, b_ref, c_ref, lam_ref, a_out, b_out, c_out,
            xh, xin, u_buf, pa, pb, ball, a16, a32, ya, za, yb, xb, zb,
-           gown, gcore, gpeer, gfin, cmid, cpart, ctot, csplat, at_buf, work, hinv, hlow, linv, gmat_a, gmat_b, c_cur,
+           gown, gcore, gpeer, gfin, cmid, cpart, ctot, csplat, at_buf, work, hinv, hlow, gpart, linv, gmat_a, gmat_b, c_cur,
            load_sem, s_ab, r_ab, s_a16, r_a16, s_a32, r_a32, s_ya, r_ya, s_za, r_za,
            s_yb, r_yb, s_xb, r_xb, s_zb, r_zb, s_g, r_g, s_c, r_c):
     tube = lax.axis_index("tube")
@@ -96,13 +91,30 @@
 
     peer_x, peer_core, peer_y = dev(tube, col, xrow), dev(tube, col, crow), dev(tube, 1 - col, row)
 
+    pair = tube + 1 - 2 * lax.rem(tube, 2)
+    mate = lax.rem(tube + 2, 4)
+    near, far = 2 - tube // 2, 3 - 3 * (tube // 2)
+    by_reach = (pair, near, far)
+    by_need = (lax.rem(pair + 2, 4), mate, pair, tube)
+
     def peer_z(d):
         return dev(shift(d), col, row)
+
+    def at_z(t):
+        return dev(t, col, row)
 
     def plane(n):
         other = lax.rem(col * 4 + row + n, 8)
         return dev(tube, other // 4, lax.rem(other, 4))
 
+    def tile(n):
+        slot = lax.rem(n, STAGES)
+        return pltpu.make_async_copy(x_ref.at[pl.ds(pl.multiple_of(n * ROWS_T, ROWS_T), ROWS_T)], xin.at[slot], load_sem.at[slot])
+
+    n_tiles = 2048 // ROWS_T
+
+    for n in range(STAGES):
+        tile(n).start()
     barrier = pltpu.get_barrier_semaphore()
     for d in range(1, 4):
         pl.semaphore_signal(barrier, inc=1, device_id=peer_z(d), device_id_type=MESH)
@@ -122,26 +134,28 @@
 
     def ab_start(v):
         own = slot_b(row, tube)
-        for d in (2, 3, 1):
-            ab_copy(v, own, d - 1, peer_z(d)).start()
         ab_copy(v, own, 3, peer_x).start()
         ab_copy(v, own, 4, peer_core).start()
-
-    def ab_relay_z(v, d):
-        slot = slot_b(row, shift(d))
+        for n in range(3):
+            ab_copy(v, own, n, at_z(by_reach[n])).start()
+
+    def ab_relay_z(v, n):
+        slot = slot_b(row, by_reach[n])
         ab_copy(v, slot, 0, peer_x).wait_recv()
-        ab_copy(v, slot, 4 + d, peer_x).start()
-        ab_copy(v, slot, 7 + d, peer_core).start()
-
-    def ab_relay_x(v, d):
-        slot = slot_b(xrow, shift(d))
+        ab_copy(v, slot, 5 + n, peer_x).start()
+        ab_copy(v, slot, 8 + n, peer_core).start()
+        return slot
+
+    def ab_relay_x(v, n):
+        slot = slot_b(xrow, tube if n == 3 else by_reach[n])
         ab_copy(v, slot, 0, peer_x).wait_recv()
-        ab_copy(v, slot, 11 + d, peer_core).start()
-
-    def ab_core(v):
-        for r in (crow, lax.rem(crow + 2, 4)):
-            for d in range(4):
-                ab_copy(v, slot_b(r, shift(d)), 0, peer_x).wait_recv()
+        ab_copy(v, slot, 11 + n, peer_core).start()
+        return slot
+
+    def ab_core(v, r, n):
+        slot = slot_b(r, tube if n == 3 else by_reach[n])
+        ab_copy(v, slot, 0, peer_x).wait_recv()
+        return slot
 
     def ab_finish(v):
         for n in range(15):
@@ -152,15 +166,15 @@
 
     def aa_start(buf, s_sem, r_sem, s):
         own = col * 4 + tube
-        for d in (2, 3, 1):
-            aa_copy(buf, s_sem, r_sem, s, own, d - 1, peer_z(d)).start()
         aa_copy(buf, s_sem, r_sem, s, own, 3, peer_y).start()
+        for n in range(3):
+            aa_copy(buf, s_sem, r_sem, s, own, n, at_z(by_reach[n])).start()
 
     def aa_relay(buf, s_sem, r_sem, s):
-        for d in (1, 3, 2):
-            slot = col * 4 + shift(d)
+        for n in range(3):
+            slot = col * 4 + by_reach[n]
             aa_copy(buf, s_sem, r_sem, s, slot, 0, peer_y).wait_recv()
-            aa_copy(buf, s_sem, r_sem, s, slot, 3 + d, peer_y).start()
+            aa_copy(buf, s_sem, r_sem, s, slot, 4 + n, peer_y).start()
 
     def aa_rest(buf, s_sem, r_sem, s):
         for d in range(4):
@@ -173,8 +187,8 @@
         lanes = lax.broadcasted_iota(jnp.int32, (RANK, RANK), 1)
         return left * right + jnp.where(rows == lanes, lam, 0.0)
 
-    def factor(left, right):
-        linv[...] = inv_chol(solve_matrix(left, right), work, hinv, hlow)
+    def factor(left, right, between=lambda: None):
+        linv[...] = inv_chol(solve_matrix(left, right), work, hinv, hlow, between)
 
     def half(q):
         return pl.ds(pl.multiple_of(q * 128, 128), 128)
@@ -190,32 +204,29 @@
     def g_link(g, device):
         return remote(gown.at[half(core)], gpeer.at[g], s_g.at[g, 1], r_g.at[g, 1], device)
 
-    def gram_b_start(v, g):
-        gown[half(core)] = jnp.zeros((128, RANK), F32)
-
-        def step(n, carry):
-            gown[half(core)] += dot16(ball[v, n, :, half(core)], ball[v, n], 0, 0)
-            return carry
-
-        lax.fori_loop(0, 16, step, 0)
-        g_link(g, peer_y).start()
-
     def g_link_wait(g, device):
         g_link(g, device).wait()
 
-    def form_u(v):
+    def take_group(v, slots, first=False):
         def step(n, carry):
-            rows = pl.ds(pl.multiple_of(n * 256, 256), 256)
-            u_buf[rows] = dot16(xh[rows], ball[v].reshape(4096, RANK), 1, 0)
+            rows = pl.ds(pl.multiple_of(n * 512, 512), 512)
+            total = None if first else u_buf[rows]
+            for slot in slots:
+                term = dot16(xh[rows, pl.ds(pl.multiple_of(slot * 256, 256), 256)], ball[v, slot], 1, 0)
+                total = term if total is None else total + term
+            u_buf[rows] = total
             return carry
 
-        lax.fori_loop(0, 8, step, 0)
-
-    def tile(n):
-        slot = lax.rem(n, STAGES)
-        return pltpu.make_async_copy(x_ref.at[pl.ds(pl.multiple_of(n * ROWS_T, ROWS_T), ROWS_T)], xin.at[slot], load_sem.at[slot])
-
-    n_tiles = 2048 // ROWS_T
+        lax.fori_loop(0, 4, step, 0)
+        for slot in slots:
+            gpart[slot] = dot16(ball[v, slot, :, half(core)], ball[v, slot], 0, 0)
+
+    def gram_b_sum(g):
+        total = gpart[0]
+        for n in range(1, 16):
+            total = total + gpart[n]
+        gown[half(core)] = total
+        g_link(g, peer_y).start()
 
     def convert(first, last):
         def step(n, carry):
@@ -228,26 +239,22 @@
         lax.fori_loop(first, last, step, 0)
 
     ball[0, slot_b(row, tube)] = b_ref[...].astype(BF16)
-    for n in range(STAGES):
-        tile(n).start()
     c_cur[...] = c_ref[...]
     ab_start(0)
     part = (n_tiles - STAGES) // 4
+    across = lax.rem(crow + 2, 4)
     convert(0, part)
-    ab_relay_z(0, 1)
-    convert(part, 2 * part)
+    ab_relay_z(0, 0)
+    ab_relay_x(0, 3)
+    convert(part, 3 * part)
     ab_relay_x(0, 0)
-    ab_relay_z(0, 3)
-    convert(2 * part, 3 * part)
-    ab_relay_z(0, 2)
-    ab_relay_x(0, 1)
     convert(3 * part, 4 * part)
     convert(4 * part, n_tiles)
-    ab_relay_x(0, 3)
-    ab_relay_x(0, 2)
-    ab_core(0)
-    gram_b_start(0, 0)
-    form_u(0)
+    take_group(0, (slot_b(row, tube), slot_b(row, pair), slot_b(xrow, tube), ab_core(0, crow, 3)), True)
+    take_group(0, (slot_b(xrow, pair), ab_relay_z(0, 1), ab_core(0, crow, 0), ab_core(0, across, 3)))
+    take_group(0, (ab_relay_z(0, 2), ab_relay_x(0, 1), ab_core(0, crow, 1), ab_core(0, across, 0)))
+    take_group(0, (ab_relay_x(0, 2), ab_core(0, crow, 2), ab_core(0, across, 1), ab_core(0, across, 2)))
+    gram_b_sum(0)
     g_link_wait(0, peer_y)
     g_swap(0, gmat_b)
     ab_finish(0)
@@ -262,8 +269,18 @@
         def ya_copy(t):
             return remote(pa.at[(1 - col) * 4 + t], ya.at[s, t], s_ya.at[s, t], r_ya.at[s, t], peer_y)
 
-        def za_copy(d):
-            return remote(pa.at[col * 4 + shift(d)], za.at[s, d - 1], s_za.at[s, d - 1], r_za.at[s, d - 1], peer_z(d))
+        def za_copy(n):
+            return remote(pa.at[col * 4 + by_need[n]], za.at[s, n], s_za.at[s, n], r_za.at[s, n], at_z(mate if n == 1 else pair))
+
+        def merge_a(n):
+            ya_copy(by_need[n]).wait_recv()
+            slot = col * 4 + by_need[n]
+            both = pa[slot] + ya[s, by_need[n]]
+            if n == 1:
+                za_copy(0).wait_recv()
+                both = both + za[s, 0]
+            pa[slot] = both
+            za_copy(n).start()
 
         def form_pa(slot):
             acc = None
@@ -272,34 +289,34 @@
                 acc = term if acc is None else acc + term
             pa[slot] = acc
 
-        for d in (2, 3, 1, 0):
-            form_pa((1 - col) * 4 + shift(d))
-            ya_copy(shift(d)).start()
-        for d in (2, 3, 1, 0):
-            form_pa(col * 4 + shift(d))
-        factor(gmat_b[...], gram_c)
-        for d in (2, 3, 1):
-            ya_copy(shift(d)).wait_recv()
-            slot = col * 4 + shift(d)
-            pa[slot] = pa[slot] + ya[s, shift(d)]
-            za_copy(d).start()
+        for n in range(4):
+            form_pa((1 - col) * 4 + by_need[n])
+            ya_copy(by_need[n]).start()
+        for n in range(4):
+            form_pa(col * 4 + by_need[n])
+        merge_a(0)
+
+        def middle_a():
+            merge_a(1)
+            merge_a(2)
+
+        factor(gmat_b[...], gram_c, middle_a)
         ya_copy(tube).wait_recv()
         total = pa[col * 4 + tube] + ya[s, tube]
-        for d in (1, 3, 2):
-            za_copy(d).wait_recv()
-            total = total + za[s, d - 1]
+        for n in (2, 1):
+            za_copy(n).wait_recv()
+            total = total + za[s, n]
         a_own = dot32(dot32(total, linv[...], 1, 1), linv[...], 1, 0)
         own_a = col * 4 + tube
         a32[s, own_a] = a_own
         a16[s, own_a] = a_own.astype(BF16)
         aa_start(a16, s_a16, r_a16, s)
-        aa_start(a32, s_a32, r_a32, s)
         for k in range(4):
             csplat[k] = jnp.broadcast_to(c_blk[k:k + 1], (128, RANK)).T
         for t in range(4):
             ya_copy(t).wait_send()
-        for d in range(1, 4):
-            za_copy(d).wait_send()
+        for n in range(3):
+            za_copy(n).wait_send()
         aa_relay(a16, s_a16, r_a16, s)
         aa_rest(a16, s_a16, r_a16, s)
         a_rows = a16[s].reshape(512, RANK)
@@ -308,6 +325,7 @@
         g = 1 + 2 * s
         core_gram = remote(gown.at[half(1 - core)], gcore.at[s], s_g.at[g, 0], r_g.at[g, 0], peer_core)
         core_gram.start()
+        aa_start(a32, s_a32, r_a32, s)
 
         def form_pb(slot):
             acc0 = acc1 = None
@@ -321,7 +339,7 @@
             pb[slot] = jnp.concatenate([acc0, acc1], axis=1)
 
         def order(n):
-            return shift((2, 3, 1, 0)[n % 4])
+            return by_need[n % 4]
 
         def chunk(n, q):
             xside = 1 - xpos if n < 4 else xpos
@@ -333,8 +351,18 @@
         def xb_copy(n):
             return remote(pb.at[chunk(n, core)], xb.at[s, n], s_xb.at[s, n], r_xb.at[s, n], peer_x)
 
-        def zb_copy(d):
-            return remote(pb.at[slot_b(row, shift(d))], zb.at[s, d - 1], s_zb.at[s, d - 1], r_zb.at[s, d - 1], peer_z(d))
+        def zb_copy(n):
+            return remote(pb.at[slot_b(row, by_need[n])], zb.at[s, n], s_zb.at[s, n], r_zb.at[s, n], at_z(mate if n == 1 else pair))
+
+        def merge_b(n):
+            xb_copy(n).wait_recv()
+            slot = slot_b(row, by_need[n])
+            both = pb[slot] + xb[s, n]
+            if n == 1:
+                zb_copy(0).wait_recv()
+                both = both + zb[s, 0]
+            pb[slot] = both
+            zb_copy(n).start()
 
         def merge_core(n):
             yb_copy(n).wait_recv()
@@ -347,28 +375,26 @@
             form_pb(chunk(n, 1 - core))
             yb_copy(n).start()
             form_pb(chunk(n, core))
-            if n == 0:
+            if n == 2:
                 core_gram.wait()
                 gown[half(core)] = gown[half(core)] + gcore[s]
                 g_link(g, peer_x).start()
             if n >= 1:
                 merge_core(n - 1)
         merge_core(7)
+        merge_b(0)
         aa_relay(a32, s_a32, r_a32, s)
         g_link_wait(g, peer_x)
         g_swap(g, gmat_a)
+        merge_b(1)
         factor(gmat_a[...], gram_c)
-        for n in range(3):
-            xb_copy(n).wait_recv()
-            slot = slot_b(row, order(n))
-            pb[slot] = pb[slot] + xb[s, n]
-            zb_copy((2, 3, 1)[n]).start()
+        merge_b(2)
         aa_rest(a32, s_a32, r_a32, s)
         xb_copy(3).wait_recv()
         total = pb[slot_b(row, tube)] + xb[s, 3]
-        for d in (1, 3, 2):
-            zb_copy(d).wait_recv()
-            total = total + zb[s, d - 1]
+        for n in (2, 1):
+            zb_copy(n).wait_recv()
+            total = total + zb[s, n]
         b_own = dot32(dot32(linv[...], total, 1, 0), linv[...], 0, 0)
         b_out[...] = b_own
         v = s + 1
@@ -378,17 +404,13 @@
             yb_copy(n).wait_send()
         for n in range(4):
             xb_copy(n).wait_send()
-        for d in range(1, 4):
-            zb_copy(d).wait_send()
-        ab_relay_z(v, 1)
-        ab_relay_z(v, 3)
-        ab_relay_x(v, 0)
-        ab_relay_z(v, 2)
-        for d in (1, 3, 2):
-            ab_relay_x(v, d)
-        ab_core(v)
-        gram_b_start(v, g + 1)
-        form_u(v)
+        for n in range(3):
+            zb_copy(n).wait_send()
+        take_group(v, (slot_b(row, tube), ab_relay_z(v, 0), ab_relay_x(v, 3), ab_core(v, crow, 3)), True)
+        take_group(v, (ab_relay_x(v, 0), ab_relay_z(v, 1), ab_core(v, crow, 0), ab_core(v, across, 3)))
+        take_group(v, (ab_relay_z(v, 2), ab_relay_x(v, 1), ab_core(v, crow, 1), ab_core(v, across, 0)))
+        take_group(v, (ab_relay_x(v, 2), ab_core(v, crow, 2), ab_core(v, across, 1), ab_core(v, across, 2)))
+        gram_b_sum(g + 1)
 
         cpart[s, 0] = jnp.zeros((8, RANK), F32)
         for k in range(4):
@@ -472,7 +494,8 @@
                 pltpu.VMEM((RANK, 512), BF16),
                 pltpu.VMEM((128, 128), F32),
                 pltpu.VMEM((2, 128, 128), F32),
-                pltpu.VMEM((2, 128, 128), F32),
+                pltpu.VMEM((128, 128), F32),
+                pltpu.VMEM((16, 128, RANK), F32),
                 pltpu.VMEM((RANK, RANK), F32),
                 pltpu.VMEM((RANK, RANK), F32),
                 pltpu.VMEM((RANK, RANK), F32),

time: 280 us -> 231 us (0.82); the launches traced: 275 us -> 231 us
  Pallas kernels: 269 us -> 225 us
    pallas_call x1, Pallas kernels: 269 us -> 225 us  [local(): pl.pallas_call(kernel, out_shape=(jax.ShapeDtypeStruct((64, RANK), F32),...]
where the time goes in v2:
time: 231 us
  Pallas kernels  225 us (97%)
  local copies, waits for them, and re-layouts  5.03 us (2%)
    pallas_call x1, Pallas kernels, local(): pl.pallas_call(kernel, out_shape=(jax.ShapeDtypeStruct((64, RANK), F32),...  225 us

profile of v2, /device:TPU:0, one launch (start us, length us, event | category | flops | bytes accessed | tf_op | source)
XLA Modules:
  0.0 231.0 jit_solution(4411013769569995377)
XLA Ops:
  1.3 0.6 broadcast_in_dim.3.lam_ref
  1.8 224.6 %shard_map.67 = (f32[64,256]{1,0:T(8,128)}, f32[256,256]{1,0:T(8,128)}, f32[16,256]{1,0:T(8,128)}) custom-call(f32[2048,4096]{1,0:T(8,128)} %bitcast.1, f32[256,256]{1,0:T(8,128)} %b_ref.1, f32[16,256]{1,0:T(8,128)} %c_ref.1, f32[1,256]{1,0:T(1,128)} %broadcast_in_dim.3.lam_ref), custom_call_target="tpu_custom_call" | custom-call | tf_op jit(solution)/shard_map/pallas_call | solution.py:463
  226.5 1.5 copy.11
  228.0 1.7 copy.12
  229.6 1.3 copy.13

commit v3 on v2

--- a/solution.py
+++ b/solution.py
@@ -24,14 +24,14 @@
     return lax.dot_general(lhs, rhs, (((lhs_dim,), (rhs_dim,)), ((), ())), preferred_element_type=F32)
 
 
-def factor_block(blk, w_ref, inv_ref, idx):
+def factor_block(blk, w_ref, inv_ref, idx, top):
     size = 128
     lane = lax.broadcasted_iota(jnp.int32, (PIV, size), 1)
     row = lax.broadcasted_iota(jnp.int32, (PIV, size), 0)
-    lanes = lax.broadcasted_iota(jnp.int32, (size, size), 1)
+    lanes = lax.broadcasted_iota(jnp.int32, (size - top, size), 1)
     lo = pl.multiple_of(blk * PIV, PIV)
     slab = w_ref[pl.ds(lo, PIV)]
-    full = w_ref[...]
+    full = w_ref[top:]
     cols = jnp.stack([jnp.broadcast_to(slab[:, q:q + 1], (PIV, size)) for q in range(PIV)])
     work = pltpu.roll(jnp.where(lane < PIV, jnp.where(lane == row, 1.0, 0.0), slab), size - PIV, 1)
     rest = pltpu.roll(jnp.where(lanes < PIV, 0.0, full), size - PIV, 1)
@@ -50,19 +50,24 @@
     mid = work * scale
     for q in range(PIV):
         rest = rest - full[:, q:q + 1] * mid[q:q + 1]
-    w_ref[...] = rest
+    w_ref[top:] = rest
     low = jnp.where(lane >= size - PIV - lo, low, 0.0)
     inv_ref[idx, pl.ds(lo, PIV)] = pltpu.roll(low, lo + PIV, 1)
 
 
+def factor_half(w_ref, inv_ref, idx):
+    for first, last in ((0, 4), (4, 8)):
+        lax.fori_loop(first, last, lambda blk, c: (factor_block(blk, w_ref, inv_ref, idx, first * PIV), c)[1], 0)
+
+
 def inv_chol(mat, w_ref, inv_ref, low_ref, between):
     w_ref[...] = mat[:128, :128]
-    lax.fori_loop(0, 128 // PIV, lambda blk, c: (factor_block(blk, w_ref, inv_ref, 0), c)[1], 0)
+    factor_half(w_ref, inv_ref, 0)
     low = dot32(mat[128:, :128], inv_ref[0], 1, 1)
     low_ref[...] = low
     w_ref[...] = mat[128:, 128:] - dot32(low, low, 1, 1)
     between()
-    lax.fori_loop(0, 128 // PIV, lambda blk, c: (factor_block(blk, w_ref, inv_ref, 1), c)[1], 0)
+    factor_half(w_ref, inv_ref, 1)
     first, second = inv_ref[0], inv_ref[1]
     off = -dot32(second, dot32(low_ref[...], first, 1, 0), 1, 0)
     top = jnp.concatenate([first, jnp.zeros((128, 128), F32)], axis=1)
@@ -207,7 +212,11 @@
     def g_link_wait(g, device):
         g_link(g, device).wait()
 
-    def take_group(v, slots, first=False):
+    def take_group(v, slots, first=False, after=lambda: None):
+        for slot in slots:
+            gpart[slot] = dot16(ball[v, slot, :, half(core)], ball[v, slot], 0, 0)
+        after()
+
         def step(n, carry):
             rows = pl.ds(pl.multiple_of(n * 512, 512), 512)
             total = None if first else u_buf[rows]
@@ -218,8 +227,6 @@
             return carry
 
         lax.fori_loop(0, 4, step, 0)
-        for slot in slots:
-            gpart[slot] = dot16(ball[v, slot, :, half(core)], ball[v, slot], 0, 0)
 
     def gram_b_sum(g):
         total = gpart[0]
@@ -253,8 +260,8 @@
     take_group(0, (slot_b(row, tube), slot_b(row, pair), slot_b(xrow, tube), ab_core(0, crow, 3)), True)
     take_group(0, (slot_b(xrow, pair), ab_relay_z(0, 1), ab_core(0, crow, 0), ab_core(0, across, 3)))
     take_group(0, (ab_relay_z(0, 2), ab_relay_x(0, 1), ab_core(0, crow, 1), ab_core(0, across, 0)))
-    take_group(0, (ab_relay_x(0, 2), ab_core(0, crow, 2), ab_core(0, across, 1), ab_core(0, across, 2)))
-    gram_b_sum(0)
+    take_group(0, (ab_relay_x(0, 2), ab_core(0, crow, 2), ab_core(0, across, 1), ab_core(0, across, 2)),
+               after=lambda: gram_b_sum(0))
     g_link_wait(0, peer_y)
     g_swap(0, gmat_b)
     ab_finish(0)
@@ -409,8 +416,9 @@
         take_group(v, (slot_b(row, tube), ab_relay_z(v, 0), ab_relay_x(v, 3), ab_core(v, crow, 3)), True)
         take_group(v, (ab_relay_x(v, 0), ab_relay_z(v, 1), ab_core(v, crow, 0), ab_core(v, across, 3)))
         take_group(v, (ab_relay_z(v, 2), ab_relay_x(v, 1), ab_core(v, crow, 1), ab_core(v, across, 0)))
-        take_group(v, (ab_relay_x(v, 2), ab_core(v, crow, 2), ab_core(v, across, 1), ab_core(v, across, 2)))
-        gram_b_sum(g + 1)
+        take_group(v, (ab_core(v, crow, 2), ab_core(v, across, 1)))
+        take_group(v, (ab_relay_x(v, 2), ab_core(v, across, 2)),
+                   after=lambda: gram_b_sum(g + 1))
 
         cpart[s, 0] = jnp.zeros((8, RANK), F32)
         for k in range(4):

time: 231 us -> 227 us (0.983)
  Pallas kernels: 225 us -> 220 us
    pallas_call x1, Pallas kernels: 225 us -> 220 us  [local(): pl.pallas_call(kernel, out_shape=(jax.ShapeDtypeStruct((64, RANK), F32),...]
where the time goes in v3:
time: 227 us
  Pallas kernels  220 us (97%)
  local copies, waits for them, and re-layouts  5.03 us (2%)
    pallas_call x1, Pallas kernels, local(): pl.pallas_call(kernel, out_shape=(jax.ShapeDtypeStruct((64, RANK), F32),...  220 us

profile of v3, /device:TPU:0, one launch (start us, length us, event | category | flops | bytes accessed | tf_op | source)
XLA Modules:
  0.0 226.6 jit_solution(8248280094653859984)
XLA Ops:
  1.3 0.6 broadcast_in_dim.3.lam_ref
  1.8 220.3 %shard_map.67 = (f32[64,256]{1,0:T(8,128)}, f32[256,256]{1,0:T(8,128)}, f32[16,256]{1,0:T(8,128)}) custom-call(f32[2048,4096]{1,0:T(8,128)} %bitcast.1, f32[256,256]{1,0:T(8,128)} %b_ref.1, f32[16,256]{1,0:T(8,128)} %c_ref.1, f32[1,256]{1,0:T(1,128)} %broadcast_in_dim.3.lam_ref), custom_call_target="tpu_custom_call" | custom-call | tf_op jit(solution)/shard_map/pallas_call | solution.py:471
  222.2 1.5 copy.11
  223.6 1.7 copy.12
  225.3 1.3 copy.13

commit v4 on v3

--- a/solution.py
+++ b/solution.py
@@ -56,7 +56,7 @@
 
 
 def factor_half(w_ref, inv_ref, idx):
-    for first, last in ((0, 4), (4, 8)):
+    for first, last in ((0, 2), (2, 4), (4, 6), (6, 8)):
         lax.fori_loop(first, last, lambda blk, c: (factor_block(blk, w_ref, inv_ref, idx, first * PIV), c)[1], 0)
 
 

time: 227 us -> 226 us (level)
  no operation moved by 1% of the time
where the time goes in v4:
time: 226 us
  Pallas kernels  219 us (97%)
  local copies, waits for them, and re-layouts  5.03 us (2%)
    pallas_call x1, Pallas kernels, local(): pl.pallas_call(kernel, out_shape=(jax.ShapeDtypeStruct((64, RANK), F32),...  219 us

profile of v4, /device:TPU:0, one launch (start us, length us, event | category | flops | bytes accessed | tf_op | source)
XLA Modules:
  0.0 225.7 jit_solution(2844702572478520617)
XLA Ops:
  1.3 0.6 broadcast_in_dim.3.lam_ref
  1.8 219.3 %shard_map.67 = (f32[64,256]{1,0:T(8,128)}, f32[256,256]{1,0:T(8,128)}, f32[16,256]{1,0:T(8,128)}) custom-call(f32[2048,4096]{1,0:T(8,128)} %bitcast.1, f32[256,256]{1,0:T(8,128)} %b_ref.1, f32[16,256]{1,0:T(8,128)} %c_ref.1, f32[1,256]{1,0:T(1,128)} %broadcast_in_dim.3.lam_ref), custom_call_target="tpu_custom_call" | custom-call | tf_op jit(solution)/shard_map/pallas_call | solution.py:471
  221.2 1.5 copy.11
  222.7 1.7 copy.12
  224.3 1.3 copy.13
